TPU v7x, 256 devices: a whole 4x4x8 slice. The times are simulated.
256 devices in a mesh: dp: 64 (over z, x_hi, y), mp: 4 (over x_lo, core).
Axes of the slice: x: 4 (x_hi: 2, x_lo: 2; x = x_hi * 2 + x_lo), y: 4, z: 8, core: 2. Of those that a mesh axis runs over, the one named last changes fastest.
Arguments:
- gradients: bfloat16 [64, 1024, 6144], P('dp', None, 'mp'), may hold values from -128 to 128
- weights: bfloat16 [1024, 6144], P(None, 'mp'), may hold values from -3 to 3
- master: float32 [1024, 6144], P('dp', 'mp'), may hold values from -6 to 6
- moment_one: float32 [1024, 6144], P('dp', 'mp'), may hold values from -6 to 6
- moment_two: float32 [1024, 6144], P('dp', 'mp'), may hold values from 0.25 to 4
- group_ids: int32 [1024], replicated, may hold values from 0 to 31, never falling along the last dimension, each value on 1 to 64 neighbouring positions
Outputs:
- new_weights: bfloat16 [1024, 6144], P(None, 'mp')
- new_master: float32 [1024, 6144], P('dp', 'mp')
- new_first: float32 [1024, 6144], P('dp', 'mp')
- new_second: float32 [1024, 6144], P('dp', 'mp')
Inputs may be any that keep to these rules, and one draw needn't show every extreme that they name: `group_ids`: group numbers never fall along the rows; each group has 1 to 64 rows and every group is present.
All inputs are finite; a program needn't handle non-finite values.
Results may differ from a plain program's by a relative error of at most 0.001.
The roundings to bfloat16 on the way count: a program that leaves them out, or rounds other values in their place, can miss the bound.
Values may be sent and summed in bfloat16 or wider, within the bound.
A program may use at most 64 MiB of HBM per device.

v0:
```python
import functools
import jax
import jax.numpy as jnp
from jax import lax
from jax.sharding import Mesh
from jax.sharding import PartitionSpec as P

DP = ("dp_0", "dp_1", "dp_2")
DP_MP = ("dp_0", "dp_1", "dp_2", "mp_0", "mp_1")
MP = ("mp_0", "mp_1")
beta_one = 0.9
beta_two = 0.999
adam_eps = 1e-06
weight_decay = 0.01
learn_rate = 0.04
step_count = 100


def split_up(x, dim, count):
    before, after = (x.shape[:dim], x.shape[dim + 1 :])
    return jnp.moveaxis(x.reshape(*before, count, -1, *after), dim, 0)


def summed_on_arrival(x, axis, dim):
    parts = split_up(x, dim, lax.axis_size(axis))
    arrived = lax.all_to_all(parts, axis, split_axis=0, concat_axis=0, tiled=True)
    return arrived.astype(jnp.float32).sum(axis=0)


def by_axis(x, axes):
    return functools.reduce(lax.psum, axes, x)


def joined_along(parts, dim):
    dims = list(parts.shape[1:])
    dims[dim] *= parts.shape[0]
    return jnp.moveaxis(parts, 0, dim).reshape(dims)


def gather_in_order(x, axes, sequence):
    parts = x[None]
    for k in sequence:
        parts = lax.all_gather(parts, axes[k], axis=0, tiled=True)
    current = [lax.axis_size(axes[k]) for k in reversed(sequence)]
    parts = parts.reshape(*current, *x.shape)
    turned = sorted(range(len(sequence)), key=lambda place: sequence[len(sequence) - 1 - place])
    return parts.transpose(*turned, *range(len(sequence), parts.ndim)).reshape(-1, *x.shape)


def whole_of(x, axes, sequence, dim):
    return joined_along(gather_in_order(x, axes, sequence), dim)


def on_device(gradients, weights, master, moment_one, moment_two, group_ids):
    owned_rows = master.shape[0]
    rows_all = weights.shape[0]
    groups = rows_all // 32
    replicas = lax.axis_size(DP)
    my_index = lax.axis_index(DP)
    first_own = my_index * owned_rows
    my_groups = lax.dynamic_slice_in_dim(group_ids, first_own, owned_rows, 0)
    member = (my_groups[:, None] == jnp.arange(groups, dtype=jnp.int32)[None, :]).astype(
        jnp.float32
    )
    weight_rows = jnp.dot(jnp.sum(master * master, axis=1), member, precision=lax.Precision.HIGHEST)
    local_grad = gradients[0]
    summed = summed_on_arrival(local_grad.astype(jnp.float32).astype(jnp.bfloat16), DP, 0)
    grad_mean = summed / replicas
    new_first = beta_one * moment_one + (1.0 - beta_one) * grad_mean
    new_second = beta_two * moment_two + (1.0 - beta_two) * grad_mean * grad_mean
    correct_one = 1.0 - beta_one**step_count
    correct_two = 1.0 - beta_two**step_count
    update = (
        new_first / correct_one / (jnp.sqrt(new_second / correct_two) + adam_eps)
        + weight_decay * master
    )
    update_rows = jnp.dot(jnp.sum(update * update, axis=1), member, precision=lax.Precision.HIGHEST)
    weight_sq, update_sq = (by_axis(weight_rows, DP_MP), by_axis(update_rows, DP_MP))
    trust_ratio = jnp.sqrt(weight_sq / (update_sq + 1e-06))
    row_ratio = jnp.dot(member, trust_ratio, precision=lax.Precision.HIGHEST)
    step_size = learn_rate * row_ratio[:, None] * update
    new_master = master - step_size
    delta_bf = (-step_size).astype(jnp.bfloat16)
    new_weights = (
        weights.astype(jnp.float32) + whole_of(delta_bf, DP, (1, 0, 2), 0).astype(jnp.float32)
    ).astype(jnp.bfloat16)
    return (new_weights, new_master, new_first, new_second)


def solution(mesh):
    torus = Mesh(mesh.devices.reshape(8, 2, 4, 2, 2), ("dp_0", "dp_1", "dp_2", "mp_0", "mp_1"))
    placed = (P(DP, None, MP), P(None, MP), P(DP, MP), P(DP, MP), P(DP, MP), P())
    return jax.shard_map(
        on_device,
        mesh=torus,
        in_specs=placed,
        out_specs=(P(None, MP), P(DP, MP), P(DP, MP), P(DP, MP)),
        check_vma=False,
    )
```

profile of v0, /device:TPU:1, one launch (start us, length us, event | category | flops | bytes accessed | tf_op | source)
XLA Modules:
  0.0 223.6 jit_solution(12461575750495941655)
XLA Ops:
  7.2 15.1 %all-to-all-start = ((bf16[64,16,1536]{2,1,0:T(8,128)(2,1)}), bf16[64,16,1536]{2,1,0:T(8,128)(2,1)S(1)}, u32[]{:S(2)}, u32[]{:S(2)}) async-start(bf16[64,16,1536]{2,1,0:T(8,128)(2,1)} %bitcast.27), calls=%async_computation | async-start | bytes 6291456 | tf_op jit(solution)/shard_map/all_to_all | solution.py:26
  22.3 0.0 copy-start.1
  22.3 0.0 all-gather.3.cloned.1.call-start
  22.4 0.8 dynamic_slice.3
  23.2 69.7 %all-to-all-done = bf16[64,16,1536]{2,1,0:T(8,128)(2,1)S(1)} async-done(((bf16[64,16,1536]{2,1,0:T(8,128)(2,1)}), bf16[64,16,1536]{2,1,0:T(8,128)(2,1)S(1)}, u32[]{:S(2)}, u32[]{:S(2)}) %all-to-all-start) | async-done | bytes 3145760 | tf_op jit(solution)/shard_map/all_to_all | solution.py:26
  92.9 0.5 convert_reduce_fusion
  93.4 0.9 multiply_reduce_fusion
  94.2 0.2 convolution_bitcast_fusion.1
  94.4 0.2 convolution_bitcast_fusion.2
  94.6 13.4 %all-reduce = (f32[32]{0:T(128)S(1)}, f32[32]{0:T(128)S(1)}) all-reduce(f32[32]{0:T(128)S(1)} %convolution_bitcast_fusion.2, f32[32]{0:T(128)S(1)} %convolution_bitcast_fusion.1), channel_id=1, replica_groups=mesh['dp_0'=8,'dp_1'=2,'dp_2'=4,'mp_0'=2,'mp_1'=2] {'dp_0'}, use_global_device_ids=true, to_apply=%region_1.0 | all-reduce | flops 64 | bytes 512 | tf_op jit(solution)/shard_map/psum | solution.py:31
  108.0 5.3 %all-reduce.4 = (f32[32]{0:T(128)S(1)}, f32[32]{0:T(128)S(1)}) all-reduce(f32[32]{0:T(128)S(1)} %get-tuple-element.4, f32[32]{0:T(128)S(1)} %get-tuple-element.5), channel_id=1, replica_groups=mesh['dp_0'=8,'dp_1'=2,'dp_2'=4,'mp_0'=2,'mp_1'=2] {'dp_1'}, use_global_device_ids=true, to_apply=%region_2.0 | all-reduce | flops 64 | bytes 512 | tf_op jit(solution)/shard_map/psum | solution.py:31
  113.3 7.7 %all-reduce.1 = (f32[32]{0:T(128)S(1)}, f32[32]{0:T(128)S(1)}) all-reduce(f32[32]{0:T(128)S(1)} %get-tuple-element.12, f32[32]{0:T(128)S(1)} %get-tuple-element.13), channel_id=1, replica_groups=mesh['dp_0'=8,'dp_1'=2,'dp_2'=4,'mp_0'=2,'mp_1'=2] {'dp_2'}, use_global_device_ids=true, to_apply=%region_3.0 | all-reduce | flops 64 | bytes 512 | tf_op jit(solution)/shard_map/psum | solution.py:31
  120.9 3.8 %all-reduce.3 = (f32[32]{0:T(128)S(1)}, f32[32]{0:T(128)S(1)}) all-reduce(f32[32]{0:T(128)S(1)} %get-tuple-element.6, f32[32]{0:T(128)S(1)} %get-tuple-element.7), channel_id=1, replica_groups=mesh['dp_0'=8,'dp_1'=2,'dp_2'=4,'mp_0'=2,'mp_1'=2] {'mp_0'}, use_global_device_ids=true, to_apply=%region_4.0 | all-reduce | flops 64 | bytes 512 | tf_op jit(solution)/shard_map/psum | solution.py:31
  124.7 11.8 %all-reduce.2 = (f32[32]{0:T(128)S(1)}, f32[32]{0:T(128)S(1)}) all-reduce(f32[32]{0:T(128)S(1)} %get-tuple-element.10, f32[32]{0:T(128)S(1)} %get-tuple-element.11), channel_id=1, replica_groups=mesh['dp_0'=8,'dp_1'=2,'dp_2'=4,'mp_0'=2,'mp_1'=2] {'mp_1'}, use_global_device_ids=true, to_apply=%region_5.0 | all-reduce | flops 64 | bytes 512 | tf_op jit(solution)/shard_map/psum | solution.py:31
  136.5 0.2 fusion.1
  136.7 0.7 multiply_subtract_fusion
  137.4 5.1 %all-gather = bf16[32,1536]{1,0:T(8,128)(2,1)S(1)} all-gather(bf16[16,1536]{1,0:T(8,128)(2,1)S(1)} %get-tuple-element.19), channel_id=2, replica_groups=mesh['dp_0'=8,'dp_1'=2,'dp_2'=4,'mp_0'=2,'mp_1'=2] {'dp_1'}, dimensions={0}, use_global_device_ids=true | all-gather | bytes 147456 | tf_op jit(solution)/shard_map/all_gather | solution.py:43
  142.5 22.8 %all_gather.10 = bf16[16,16,1536]{2,1,0:T(8,128)(2,1)} all-gather(bf16[2,16,1536]{2,1,0:T(8,128)(2,1)S(1)} %bitcast.29), channel_id=1, replica_groups=mesh['dp_0'=8,'dp_1'=2,'dp_2'=4,'mp_0'=2,'mp_1'=2] {'dp_0'}, dimensions={0}, use_global_device_ids=true | all-gather | bytes 884736 | tf_op jit(solution)/shard_map/all_gather | solution.py:43
  165.3 0.0 all-gather.3.cloned.1.call-update
  165.4 44.0 %all-gather.3.cloned.1.call-done = bf16[64,16,1536]{2,1,0:T(8,128)(2,1)} async-done(((bf16[16,16,1536]{2,1,0:T(8,128)(2,1)}), bf16[64,16,1536]{2,1,0:T(8,128)(2,1)}) %all-gather.3.cloned.1.call-update) | async-done | bytes 3145744 | tf_op jit(solution)/shard_map/all_gather | solution.py:43
  209.4 2.8 %convert_bitcast_fusion = f32[8,2,4,16,1536]{4,3,1,0,2:T(8,128)S(1)} fusion(bf16[4,8,2,16,1536]{4,3,2,1,0:T(8,128)(2,1)} %bitcast.28), kind=kLoop, calls=%fused_computation | loop fusion | flops 1572864 | bytes 9437184 | tf_op jit(solution)/shard_map/convert_element_type | solution.py:85
  212.2 0.4 copy.11
  212.6 1.4 copy-done
  214.1 2.7 %fusion = bf16[1024,1536]{1,0:T(8,128)(2,1)} fusion(f32[8,2,4,16,1536]{4,3,2,1,0:T(8,128)S(1)} %copy.11, bf16[1024,1536]{1,0:T(8,128)(2,1)S(1)} %copy-done), kind=kLoop, calls=%fused_computation.2 | loop fusion | flops 4718592 | bytes 12582912 | tf_op jit(solution)/shard_map/convert_element_type | solution.py:86
  (6 shorter events, 0.0 us)
Async XLA Ops:
  7.2 85.7 %all-to-all-start = ((bf16[64,16,1536]{2,1,0:T(8,128)(2,1)}), bf16[64,16,1536]{2,1,0:T(8,128)(2,1)S(1)}, u32[]{:S(2)}, u32[]{:S(2)}) async-start(bf16[64,16,1536]{2,1,0:T(8,128)(2,1)} %bitcast.27), calls=%async_computation | async-start | bytes 6291456 | tf_op jit(solution)/shard_map/all_to_all | solution.py:26
  22.3 71.1 %copy-start.1 = (f32[16,1536]{1,0:T(8,128)S(1)}, f32[16,1536]{1,0:T(8,128)}, u32[]{:S(2)}) copy-start(f32[16,1536]{1,0:T(8,128)} %param.8) | copy-start | bytes 294916
  22.3 71.1 %copy-start.2 = (f32[16,1536]{1,0:T(8,128)S(1)}, f32[16,1536]{1,0:T(8,128)}, u32[]{:S(2)}) copy-start(f32[16,1536]{1,0:T(8,128)} %param.9) | copy-start | bytes 294916
  22.3 71.1 %copy-start.3 = (f32[16,1536]{1,0:T(8,128)S(1)}, f32[16,1536]{1,0:T(8,128)}, u32[]{:S(2)}) copy-start(f32[16,1536]{1,0:T(8,128)} %param.10) | copy-start | bytes 294916
  22.3 187.1 %all-gather.3.cloned.1.call-start = ((), (), s32[]{:S(2)}) async-start(), calls=%async_computation.1 | async-start | bytes 3932160 | tf_op jit(solution)/shard_map/all_gather | solution.py:43
  212.2 1.9 copy-start
Sparse Core Ops, SparseCore 0:
  165.5 43.8 all-gather.2
where the time goes:
time: 224 us
  waiting for transfers between devices  114 us (51%)
  blocking collectives  69.8 us (31%)
  starting transfers between devices  15.2 us (7%)
  between operations  14.1 us (6%)
  other arithmetic  7.49 us (3%)
  local copies, waits for them, and re-layouts  2.71 us (1%)
    all_to_all x1, waiting for transfers between devices, summed_on_arrival(): lax.all_to_all(parts, axis, split_axis=0, concat_axis=0, tiled=True)  69.7 us
    all_gather x1, waiting for transfers between devices, gather_in_order(): parts = lax.all_gather(parts, axes[k], axis=0, tiled=True)  44 us
    psum x5, blocking collectives, by_axis(): return functools.reduce(lax.psum, axes, x)  41.9 us
    all_gather x2, blocking collectives, gather_in_order(): parts = lax.all_gather(parts, axes[k], axis=0, tiled=True)  27.9 us
    all_to_all x1, starting transfers between devices, summed_on_arrival(): lax.all_to_all(parts, axis, split_axis=0, concat_axis=0, tiled=True)  15.1 us
  transfers between devices with their start and end apart: 2, of which 2 were waited for; matrix products, arithmetic and copies ran while one was open for 0% of the time, Pallas kernels for 0%

commit v1 on v0

--- a/solution.py
+++ b/solution.py
@@ -40,7 +40,9 @@
 def gather_in_order(x, axes, sequence):
     parts = x[None]
     for k in sequence:
-        parts = lax.all_gather(parts, axes[k], axis=0, tiled=True)
+        parts = jnp.concatenate(
+            lax.all_to_all(jnp.stack([parts] * lax.axis_size(axes[k])), axes[k], 0, 0), axis=0
+        )
     current = [lax.axis_size(axes[k]) for k in reversed(sequence)]
     parts = parts.reshape(*current, *x.shape)
     turned = sorted(range(len(sequence)), key=lambda place: sequence[len(sequence) - 1 - place])

time: 224 us -> 209 us (0.933); the launches traced: 224 us -> 206 us
  waiting for transfers between devices: 114 us -> 69.7 us
  blocking collectives: 69.8 us -> 111 us
  between operations: 14.1 us -> 0.74 us
    all_to_all x0 -> x3, blocking collectives: none -> 69.1 us  [gather_in_order(): lax.all_to_all(jnp.stack([parts] * lax.axis_size(axes[k])), axes[k], 0, 0)]
    all_gather x1 -> x0, waiting for transfers between devices: 44 us -> none  [gather_in_order(): parts = lax.all_gather(parts, axes[k], axis=0, tiled=True)]
    all_gather x2 -> x0, blocking collectives: 27.9 us -> none  [gather_in_order(): parts = lax.all_gather(parts, axes[k], axis=0, tiled=True)]
  transfers between devices with their start and end apart: 2 -> 1, of which waited for: 2 -> 1; matrix products, arithmetic and copies ran while one was open for 0% -> 0% of each run, Pallas kernels for 0% -> 0%
where the time goes in v1:
time: 209 us; the launch traced here: 206 us
  blocking collectives  111 us (53%)
  waiting for transfers between devices  69.7 us (33%)
  starting transfers between devices  15.1 us (7%)
  other arithmetic  5.61 us (3%)
  local copies, waits for them, and re-layouts  3.17 us (2%)
    all_to_all x1, waiting for transfers between devices, summed_on_arrival(): lax.all_to_all(parts, axis, split_axis=0, concat_axis=0, tiled=True)  69.7 us
    all_to_all x3, blocking collectives, gather_in_order(): lax.all_to_all(jnp.stack([parts] * lax.axis_size(axes[k])), axes[k], 0, 0)  69.1 us
    psum x5, blocking collectives, by_axis(): return functools.reduce(lax.psum, axes, x)  41.9 us
    all_to_all x1, starting transfers between devices, summed_on_arrival(): lax.all_to_all(parts, axis, split_axis=0, concat_axis=0, tiled=True)  15.1 us
  transfers between devices with their start and end apart: 1, of which 1 were waited for; matrix products, arithmetic and copies ran while one was open for 0% of the time, Pallas kernels for 0%

profile of v1, /device:TPU:1, one launch (start us, length us, event | category | flops | bytes accessed | tf_op | source)
XLA Modules:
  0.0 205.9 jit_solution(12981610433176750513)
XLA Ops:
  0.6 15.1 %all-to-all-start = ((bf16[64,16,1536]{2,1,0:T(8,128)(2,1)}), bf16[64,16,1536]{2,1,0:T(8,128)(2,1)S(1)}, u32[]{:S(2)}, u32[]{:S(2)}) async-start(bf16[64,16,1536]{2,1,0:T(8,128)(2,1)} %bitcast.31), calls=%async_computation | async-start | bytes 6291456 | tf_op jit(solution)/shard_map/all_to_all | solution.py:26
  15.8 0.0 copy-start.1
  15.8 0.8 dynamic_slice.3
  16.6 69.7 %all-to-all-done = bf16[64,16,1536]{2,1,0:T(8,128)(2,1)S(1)} async-done(((bf16[64,16,1536]{2,1,0:T(8,128)(2,1)}), bf16[64,16,1536]{2,1,0:T(8,128)(2,1)S(1)}, u32[]{:S(2)}, u32[]{:S(2)}) %all-to-all-start) | async-done | bytes 3145760 | tf_op jit(solution)/shard_map/all_to_all | solution.py:26
  86.4 0.5 convert_reduce_fusion
  86.8 0.9 multiply_reduce_fusion
  87.7 0.2 convolution_bitcast_fusion.1
  87.9 0.2 convolution_bitcast_fusion.2
  88.1 13.4 %all-reduce = (f32[32]{0:T(128)S(1)}, f32[32]{0:T(128)S(1)}) all-reduce(f32[32]{0:T(128)S(1)} %convolution_bitcast_fusion.2, f32[32]{0:T(128)S(1)} %convolution_bitcast_fusion.1), channel_id=1, replica_groups=mesh['dp_0'=8,'dp_1'=2,'dp_2'=4,'mp_0'=2,'mp_1'=2] {'dp_0'}, use_global_device_ids=true, to_apply=%region_1.0 | all-reduce | flops 64 | bytes 512 | tf_op jit(solution)/shard_map/psum | solution.py:31
  101.5 5.3 %all-reduce.4 = (f32[32]{0:T(128)S(1)}, f32[32]{0:T(128)S(1)}) all-reduce(f32[32]{0:T(128)S(1)} %get-tuple-element.4, f32[32]{0:T(128)S(1)} %get-tuple-element.5), channel_id=1, replica_groups=mesh['dp_0'=8,'dp_1'=2,'dp_2'=4,'mp_0'=2,'mp_1'=2] {'dp_1'}, use_global_device_ids=true, to_apply=%region_2.0 | all-reduce | flops 64 | bytes 512 | tf_op jit(solution)/shard_map/psum | solution.py:31
  106.7 7.7 %all-reduce.1 = (f32[32]{0:T(128)S(1)}, f32[32]{0:T(128)S(1)}) all-reduce(f32[32]{0:T(128)S(1)} %get-tuple-element.12, f32[32]{0:T(128)S(1)} %get-tuple-element.13), channel_id=1, replica_groups=mesh['dp_0'=8,'dp_1'=2,'dp_2'=4,'mp_0'=2,'mp_1'=2] {'dp_2'}, use_global_device_ids=true, to_apply=%region_3.0 | all-reduce | flops 64 | bytes 512 | tf_op jit(solution)/shard_map/psum | solution.py:31
  114.4 3.8 %all-reduce.3 = (f32[32]{0:T(128)S(1)}, f32[32]{0:T(128)S(1)}) all-reduce(f32[32]{0:T(128)S(1)} %get-tuple-element.6, f32[32]{0:T(128)S(1)} %get-tuple-element.7), channel_id=1, replica_groups=mesh['dp_0'=8,'dp_1'=2,'dp_2'=4,'mp_0'=2,'mp_1'=2] {'mp_0'}, use_global_device_ids=true, to_apply=%region_4.0 | all-reduce | flops 64 | bytes 512 | tf_op jit(solution)/shard_map/psum | solution.py:31
  118.2 11.8 %all-reduce.2 = (f32[32]{0:T(128)S(1)}, f32[32]{0:T(128)S(1)}) all-reduce(f32[32]{0:T(128)S(1)} %get-tuple-element.10, f32[32]{0:T(128)S(1)} %get-tuple-element.11), channel_id=1, replica_groups=mesh['dp_0'=8,'dp_1'=2,'dp_2'=4,'mp_0'=2,'mp_1'=2] {'mp_1'}, use_global_device_ids=true, to_apply=%region_5.0 | all-reduce | flops 64 | bytes 512 | tf_op jit(solution)/shard_map/psum | solution.py:31
  130.0 0.2 fusion.1
  130.2 0.7 multiply_subtract_fusion
  130.9 8.4 %all_to_all.20 = bf16[2,1,16,1536]{3,2,1,0:T(8,128)(2,1)S(1)} all-to-all(bf16[2,1,16,1536]{3,2,1,0:T(8,128)(2,1)S(1)} %pad_maximum_fusion), channel_id=1, replica_groups=mesh['dp_0'=8,'dp_1'=2,'dp_2'=4,'mp_0'=2,'mp_1'=2] {'dp_1'}, dimensions={0} | all-to-all | bytes 196608 | tf_op jit(solution)/shard_map/all_to_all | solution.py:44
  139.4 0.1 stack.10
  139.4 24.2 %all_to_all.21 = bf16[8,2,16,1536]{3,2,1,0:T(8,128)(2,1)S(1)} all-to-all(bf16[8,2,16,1536]{3,2,1,0:T(8,128)(2,1)S(1)} %stack.10), channel_id=1, replica_groups=mesh['dp_0'=8,'dp_1'=2,'dp_2'=4,'mp_0'=2,'mp_1'=2] {'dp_0'}, dimensions={0} | all-to-all | bytes 1572864 | tf_op jit(solution)/shard_map/all_to_all | solution.py:44
  163.6 0.4 stack.11
  164.0 36.4 %all_to_all.22 = bf16[4,16,16,1536]{3,2,1,0:T(8,128)(2,1)S(1)} all-to-all(bf16[4,16,16,1536]{3,2,1,0:T(8,128)(2,1)S(1)} %stack.11), channel_id=1, replica_groups=mesh['dp_0'=8,'dp_1'=2,'dp_2'=4,'mp_0'=2,'mp_1'=2] {'dp_2'}, dimensions={0} | all-to-all | bytes 6291456 | tf_op jit(solution)/shard_map/all_to_all | solution.py:44
  200.4 0.9 convert_bitcast_fusion
  201.3 0.4 copy.10
  201.8 1.4 copy-done
  203.2 2.7 %fusion = bf16[1024,1536]{1,0:T(8,128)(2,1)} fusion(f32[8,2,4,16,1536]{4,3,2,1,0:T(8,128)S(1)} %copy.10, bf16[1024,1536]{1,0:T(8,128)(2,1)S(1)} %copy-done), kind=kLoop, calls=%fused_computation.2 | loop fusion | flops 4718592 | bytes 12582912 | tf_op jit(solution)/shard_map/convert_element_type | solution.py:88
  (7 shorter events, 0.0 us)
Async XLA Ops:
  0.6 85.7 %all-to-all-start = ((bf16[64,16,1536]{2,1,0:T(8,128)(2,1)}), bf16[64,16,1536]{2,1,0:T(8,128)(2,1)S(1)}, u32[]{:S(2)}, u32[]{:S(2)}) async-start(bf16[64,16,1536]{2,1,0:T(8,128)(2,1)} %bitcast.31), calls=%async_computation | async-start | bytes 6291456 | tf_op jit(solution)/shard_map/all_to_all | solution.py:26
  15.8 71.1 %copy-start.1 = (f32[16,1536]{1,0:T(8,128)S(1)}, f32[16,1536]{1,0:T(8,128)}, u32[]{:S(2)}) copy-start(f32[16,1536]{1,0:T(8,128)} %param.8) | copy-start | bytes 294916
  15.8 71.1 %copy-start.2 = (f32[16,1536]{1,0:T(8,128)S(1)}, f32[16,1536]{1,0:T(8,128)}, u32[]{:S(2)}) copy-start(f32[16,1536]{1,0:T(8,128)} %param.9) | copy-start | bytes 294916
  15.8 71.1 %copy-start.3 = (f32[16,1536]{1,0:T(8,128)S(1)}, f32[16,1536]{1,0:T(8,128)}, u32[]{:S(2)}) copy-start(f32[16,1536]{1,0:T(8,128)} %param.10) | copy-start | bytes 294916
  201.3 1.9 copy-start
